TPU v7x, 256 devices: a whole 4x4x8 slice. The times are simulated.
256 devices in a mesh: agent: 128 (over x, y, z), grid: 2 (over core).
Axes of the slice: x: 4, y: 4, z: 8, core: 2. Of those that a mesh axis runs over, the one named last changes fastest.
Arguments:
- value_prior: float32 [2048, 1024], P(None, 'agent'), may hold values from -6 to 6
- trans_weight: float32 [128, 128], replicated, may hold values from 0.05 to 1
- perceived_law_coefficient: float32 [4], replicated, may hold values from 0.7 to 1
- perceived_law_constant: float32 [4], replicated, may hold values from 0.5 to 4
- interest: float32 [4, 16], replicated, may hold values from 0 to 0.05
- wage_level: float32 [4, 16], replicated, may hold values from 0.5 to 1.5
- efficiency: float32 [32], replicated, may hold values from 0.2 to 3
- holdings: float32 [1048576], P('agent'), may hold values from 0 to 40
- shocks: int32 [4, 1048576], P(None, 'agent'), may hold values from 0 to 31
- brackets: int32 [4, 1048576], P(None, 'agent'), may hold values from 0 to 1022
- aggregate: int32 [4], replicated, may hold values from 0 to 3
Outputs:
- value_new: float32 [2048, 1024], P('agent', 'grid')
- policy: float32 [2048, 1024], P('agent', 'grid')
- holdings_final: float32 [1048576], P('agent')
- capital: float32 [4], replicated
All inputs are finite; a program needn't handle non-finite values.
Results may differ from a plain program's by a relative error of at most 0.0003.
Values sent between devices are 32-bit elements; how exact they have to be, the bound alone decides.
A program may use at most 64 MiB of HBM per device.

v0:
```python
import jax
import jax.numpy as jnp
from jax import lax
from jax.sharding import Mesh
from jax.sharding import PartitionSpec as P

A = 1024
E = 32
NK = 16
Z = 4
STATES = 2048
PERIODS = 4
AGENT = ("agent_0", "agent_1", "agent_2")
wealth_upper_limit = 40.0
beta_disc = 0.96
tau_soft = 0.02
floor_cons = 0.1
highest = lax.Precision.HIGHEST


def laid_out(parts, dim):
    parts = jnp.moveaxis(parts, 0, dim)
    shape = parts.shape
    return parts.reshape(*shape[:dim], shape[dim] * shape[dim + 1], *shape[dim + 2 :])


def sent_to_all(x, axis):
    copies = jnp.broadcast_to(x, (lax.axis_size(axis), *x.shape))
    return lax.all_to_all(copies, axis, split_axis=0, concat_axis=0, tiled=True)


def gathered_copies(x, axis, dim):
    return laid_out(sent_to_all(x, axis), dim)


def over_axes(x, axes):
    for axis in axes:
        x = lax.psum(x, axis)
    return x


def make_points():
    fraction = jnp.arange(A, dtype=jnp.float32) / (A - 1)
    return wealth_upper_limit * fraction * fraction


def hat_function_shares(position):
    spacing = wealth_upper_limit / (NK - 1)
    savings_mesh_points = wealth_upper_limit * jnp.arange(NK, dtype=jnp.float32) / (NK - 1)
    return jnp.maximum(0.0, 1.0 - jnp.abs(position[..., None] - savings_mesh_points) / spacing)


def one_hot(indices, number):
    return (indices[:, None] == jnp.arange(number, dtype=jnp.int32)[None, :]).astype(jnp.float32)


def state_parts(states):
    zone_of = states // (NK * E)
    level_of = states // E % NK
    kind_of = states % E
    return (zone_of, level_of, kind_of)


def expect_rows(rows_in, transition, offset_coefficients):
    columns = rows_in.shape[1]
    value_cube = rows_in.reshape(Z, NK, E, columns)
    blended = jnp.einsum(
        "zeyf,ykfn->zekn", transition.reshape(Z, E, Z, E), value_cube, precision=highest
    )
    result = jnp.einsum("zjk,zekn->zjen", offset_coefficients, blended, precision=highest)
    return result.reshape(STATES, columns)


def bellman(points, wealth, expected):
    consume = wealth[:, None] - points[None, :]
    clipped = jnp.maximum(consume, floor_cons)
    utility = jnp.log(clipped) + (consume - clipped) / floor_cons
    scores = (utility + beta_disc * expected[None, :]) / tau_soft
    highest_score = jnp.max(scores, axis=1, keepdims=True)
    weight = jnp.exp(scores - highest_score)
    totals = jnp.sum(weight, axis=1)
    values_now = tau_soft * (highest_score[:, 0] + jnp.log(totals))
    chosen = jnp.sum(weight * points[None, :], axis=1) / totals
    return (values_now, chosen)


def advance(lookup, points, current, shock_row, bracket_row):
    flattened = lookup.reshape(-1)
    flat_index = shock_row * lookup.shape[1] + bracket_row
    value_low = jnp.take(flattened, flat_index)
    value_high = jnp.take(flattened, flat_index + 1)
    edge_low = jnp.take(points, bracket_row)
    edge_high = jnp.take(points, bracket_row + 1)
    fraction = jnp.clip((current - edge_low) / (edge_high - edge_low), 0.0, 1.0)
    return value_low + fraction * (value_high - value_low)


def on_device(
    value_prior,
    trans_weight,
    perceived_law_coefficient,
    perceived_law_constant,
    interest,
    wage_level,
    efficiency,
    holdings,
    shocks,
    brackets,
    aggregate,
):
    agent_count = lax.axis_size(AGENT)
    per_device = STATES // agent_count
    half_rows = A // lax.axis_size("grid")
    first_state = lax.axis_index(AGENT) * per_device
    own_states = first_state + jnp.arange(per_device, dtype=jnp.int32)
    points = make_points()
    transition = trans_weight / jnp.sum(trans_weight, axis=1, keepdims=True)
    savings_mesh_points = wealth_upper_limit * jnp.arange(NK, dtype=jnp.float32) / (NK - 1)
    predicted_stock = jnp.clip(
        perceived_law_coefficient[:, None] * savings_mesh_points[None, :]
        + perceived_law_constant[:, None],
        0.0,
        wealth_upper_limit,
    )
    offset_coefficients = hat_function_shares(predicted_stock)
    partial_value = expect_rows(value_prior, transition, offset_coefficients)
    expected = lax.all_to_all(partial_value, AGENT, split_axis=0, concat_axis=1, tiled=True)
    zone_of, level_of, kind_of = state_parts(own_states)
    price_hot = one_hot(zone_of * NK + level_of, Z * NK)
    interest_own = jnp.sum(price_hot * interest.reshape(1, Z * NK), axis=1)
    wage_own = jnp.sum(price_hot * wage_level.reshape(1, Z * NK), axis=1)
    kind_hot = one_hot(kind_of, E)
    efficiency_own = jnp.sum(kind_hot * efficiency[None, :], axis=1)
    growth = 1.0 + interest_own
    income = wage_own * efficiency_own
    own_points = lax.dynamic_slice_in_dim(points, lax.axis_index("grid") * half_rows, half_rows)

    def one_state(packed):
        column, factor, earned = packed
        return bellman(points, own_points * factor + earned, column)

    values_now, policy = lax.map(one_state, (expected, growth, income))
    agents_total = holdings.shape[0] * agent_count
    halves_in = gathered_copies(policy, "grid", 1)
    policy_cube = lax.all_gather(halves_in, AGENT, axis=0, tiled=True).reshape(Z, NK, E, A)
    current = holdings
    capital_path = []
    for period in range(PERIODS):
        capital = over_axes(jnp.sum(current), AGENT) / agents_total
        capital_path.append(capital)
        knot_weights = hat_function_shares(capital)
        sliced = lax.dynamic_index_in_dim(policy_cube, aggregate[period], 0, keepdims=False)
        lookup = jnp.einsum("k,kea->ea", knot_weights, sliced, precision=highest)
        current = advance(lookup, points, current, shocks[period], brackets[period])
    return (values_now, policy, current, jnp.stack(capital_path))


def solution(mesh):
    finer = Mesh(
        mesh.devices.reshape(4, 4, 8, mesh.shape["grid"]), ("agent_0", "agent_1", "agent_2", "grid")
    )
    in_specs = (
        P(None, AGENT),
        P(),
        P(),
        P(),
        P(),
        P(),
        P(),
        P(AGENT),
        P(None, AGENT),
        P(None, AGENT),
        P(),
    )
    out_specs = (P(AGENT, "grid"), P(AGENT, "grid"), P(AGENT), P())
    return jax.shard_map(
        on_device, mesh=finer, in_specs=in_specs, out_specs=out_specs, check_vma=False
    )
```

profile of v0, /device:TPU:8, one launch (start us, length us, event | category | flops | bytes accessed | tf_op | source)
XLA Modules:
  0.0 961.3 jit_solution(12016140227608750191)
XLA Ops:
  13.5 15.3 %all-to-all-start = ((f32[128,1,128]{2,1,0:T(1,128)}), f32[128,1,128]{2,1,0:T(1,128)S(1)}, u32[]{:S(2)}, u32[]{:S(2)}) async-start(f32[128,1,128]{2,1,0:T(1,128)} %reshape.401), calls=%async_computation | async-start | bytes 131072 | tf_op jit(solution)/shard_map/all_to_all | solution.py:127
  29.6 10.3 %all-to-all-done = f32[128,1,128]{2,1,0:T(1,128)S(1)} async-done(((f32[128,1,128]{2,1,0:T(1,128)}), f32[128,1,128]{2,1,0:T(1,128)S(1)}, u32[]{:S(2)}, u32[]{:S(2)}) %all-to-all-start) | async-done | bytes 65568 | tf_op jit(solution)/shard_map/all_to_all | solution.py:127
  41.7 98.6 %while.14 = (s32[]{:T(128)}, f32[16,512]{1,0:T(8,128)}, f32[16,512]{1,0:T(8,128)S(1)}, f32[16]{0:T(128)S(1)}, f32[512]{0:T(512)S(1)}, /*index=5*/f32[16]{0:T(128)S(1)}, f32[16,1024]{1,0:T(8,128)S(1)}, s32[]{:T(128)}, s32[]{:T(128)}) while((s32[]{:T(128)}, f32[16,512]{1,0:T(8,128)}, f32[16,512]{1,0:T(8,128)S(1)}, ...), condition=%wide.region_8.9_spmd.clone.clone, body=%wide.region_4.8_spmd.clone.clone.sunk | while | flops 9966594 | bytes 63633 | solution.py:142
  45.1 1.4 multiply_reduce_fusion.2
  46.5 1.3 dynamic_update_slice.13
  51.2 1.4 multiply_reduce_fusion.2
  52.6 1.3 dynamic_update_slice.13
  57.4 1.4 multiply_reduce_fusion.2
  58.8 1.3 dynamic_update_slice.13
  63.6 1.4 multiply_reduce_fusion.2
  64.9 1.3 dynamic_update_slice.13
  69.7 1.4 multiply_reduce_fusion.2
  75.9 1.4 multiply_reduce_fusion.2
  82.1 1.4 multiply_reduce_fusion.2
  88.2 1.4 multiply_reduce_fusion.2
  89.6 1.3 dynamic_update_slice.13
  94.4 1.4 multiply_reduce_fusion.2
  95.8 1.3 dynamic_update_slice.13
  100.5 1.4 multiply_reduce_fusion.2
  101.9 1.3 dynamic_update_slice.13
  106.7 1.4 multiply_reduce_fusion.2
  108.1 1.3 dynamic_update_slice.13
  112.9 1.4 multiply_reduce_fusion.2
  114.2 1.3 dynamic_update_slice.13
  119.0 1.4 multiply_reduce_fusion.2
  125.2 1.4 multiply_reduce_fusion.2
  131.4 1.4 multiply_reduce_fusion.2
  137.5 1.4 multiply_reduce_fusion.2
  140.3 3.8 all_to_all.24
  145.4 9.0 psum.84
  154.4 9.8 %psum.85 = f32[]{:T(128)} all-reduce(f32[]{:T(128)} %psum.84), channel_id=1, replica_groups=mesh['agent_0'=4,'agent_1'=4,'agent_2'=8,'grid'=2] {'agent_1'}, use_global_device_ids=true, to_apply=%region_11.12 | all-reduce | flops 1 | bytes 8 | tf_op jit(solution)/shard_map/psum | solution.py:38
  164.2 15.9 %psum.86 = f32[]{:T(128)} all-reduce(f32[]{:T(128)} %psum.85), channel_id=1, replica_groups=mesh['agent_0'=4,'agent_1'=4,'agent_2'=8,'grid'=2] {'agent_2'}, use_global_device_ids=true, to_apply=%region_12.13 | all-reduce | flops 1 | bytes 8 | tf_op jit(solution)/shard_map/psum | solution.py:38
  186.2 32.9 %gather_fusion.2 = f32[8192]{0:T(1024)S(1)} fusion(f32[1024]{0:T(1024)S(1)} %fusion.55, s32[8192]{0:T(1024)S(1)} %get-tuple-element.165), kind=kCustom, calls=%fused_computation.9.clone | custom fusion | bytes 98304 | tf_op jit(solution)/shard_map/jit(_take)/gather | solution.py:93
  219.1 32.9 %gather_fusion.1 = f32[8192]{0:T(1024)S(1)} fusion(f32[1024]{0:T(1024)S(1)} %fusion.55, s32[8192]{0:T(1024)S(1)} %get-tuple-element.166), kind=kCustom, calls=%fused_computation.1.clone | custom fusion | bytes 98304 | tf_op jit(solution)/shard_map/jit(_take)/gather | solution.py:92
  252.1 32.9 %gather_fusion.6 = f32[8192]{0:T(1024)S(1)} fusion(f32[1024]{0:T(1024)S(1)} %fusion.55, s32[8192]{0:T(1024)S(1)} %get-tuple-element.163), kind=kCustom, calls=%fused_computation.11.clone | custom fusion | bytes 98304 | tf_op jit(solution)/shard_map/jit(_take)/gather | solution.py:93
  284.9 32.9 %gather_fusion.5 = f32[8192]{0:T(1024)S(1)} fusion(f32[1024]{0:T(1024)S(1)} %fusion.55, s32[8192]{0:T(1024)S(1)} %get-tuple-element.164), kind=kCustom, calls=%fused_computation.10.clone | custom fusion | bytes 98304 | tf_op jit(solution)/shard_map/jit(_take)/gather | solution.py:92
  317.9 32.9 %gather_fusion.10 = f32[8192]{0:T(1024)S(1)} fusion(f32[1024]{0:T(1024)S(1)} %fusion.55, s32[8192]{0:T(1024)S(1)} %get-tuple-element.161), kind=kCustom, calls=%fused_computation.13.clone | custom fusion | bytes 98304 | tf_op jit(solution)/shard_map/jit(_take)/gather | solution.py:93
  354.0 6.7 constant_dynamic-slice_fusion.3
  363.0 45.5 %gather_fusion.3 = f32[8192]{0:T(1024)S(1)} fusion(f32[32768]{0:T(1024)S(1)} %bitcast.106, s32[8192]{0:T(1024)S(1)} %get-tuple-element.156), kind=kCustom, calls=%fused_computation.2.clone | custom fusion | bytes 98304 | tf_op jit(solution)/shard_map/jit(_take)/gather | solution.py:91
  408.6 45.5 %gather_fusion = f32[8192]{0:T(1024)S(1)} fusion(f32[32768]{0:T(1024)S(1)} %bitcast.107, s32[8192]{0:T(1024)S(1)} %get-tuple-element.155), kind=kCustom, calls=%fused_computation.clone | custom fusion | bytes 98304 | tf_op jit(solution)/shard_map/jit(_take)/gather | solution.py:90
  454.8 9.4 psum.87
  464.2 32.9 %gather_fusion.9 = f32[8192]{0:T(1024)S(1)} fusion(f32[1024]{0:T(1024)S(1)} %fusion.55, s32[8192]{0:T(1024)S(1)} %get-tuple-element.162), kind=kCustom, calls=%fused_computation.12.clone | custom fusion | bytes 98304 | tf_op jit(solution)/shard_map/jit(_take)/gather | solution.py:92
  497.1 9.5 psum.88
  506.5 4.2 copy.36
  510.7 16.2 %psum.89 = f32[]{:T(128)} all-reduce(f32[]{:T(128)} %psum.88), channel_id=1, replica_groups=mesh['agent_0'=4,'agent_1'=4,'agent_2'=8,'grid'=2] {'agent_2'}, use_global_device_ids=true, to_apply=%region_16.19 | all-reduce | flops 1 | bytes 8 | tf_op jit(solution)/shard_map/psum | solution.py:38
  527.5 2.7 fusion.62
  530.2 45.5 %gather_fusion.7 = f32[8192]{0:T(1024)S(1)} fusion(f32[32768]{0:T(1024)S(1)} %bitcast.108, s32[8192]{0:T(1024)S(1)} %get-tuple-element.154), kind=kCustom, calls=%fused_computation.4.clone | custom fusion | bytes 98304 | tf_op jit(solution)/shard_map/jit(_take)/gather | solution.py:91
  575.8 45.5 %gather_fusion.4 = f32[8192]{0:T(1024)S(1)} fusion(f32[32768]{0:T(1024)S(1)} %bitcast.109, s32[8192]{0:T(1024)S(1)} %get-tuple-element.153), kind=kCustom, calls=%fused_computation.3.clone | custom fusion | bytes 98304 | tf_op jit(solution)/shard_map/jit(_take)/gather | solution.py:90
  622.0 9.2 psum.90
  631.2 32.9 %gather_fusion.14 = f32[8192]{0:T(1024)S(1)} fusion(f32[1024]{0:T(1024)S(1)} %fusion.55, s32[8192]{0:T(1024)S(1)} %get-tuple-element.158), kind=kCustom, calls=%fused_computation.15.clone | custom fusion | bytes 98304 | tf_op jit(solution)/shard_map/jit(_take)/gather | solution.py:93
  664.1 9.0 psum.91
  673.1 4.2 copy.37
  677.2 16.0 %psum.92 = f32[]{:T(128)} all-reduce(f32[]{:T(128)} %psum.91), channel_id=1, replica_groups=mesh['agent_0'=4,'agent_1'=4,'agent_2'=8,'grid'=2] {'agent_2'}, use_global_device_ids=true, to_apply=%region_20.23 | all-reduce | flops 1 | bytes 8 | tf_op jit(solution)/shard_map/psum | solution.py:38
  693.9 2.7 fusion.60
  696.6 45.5 %gather_fusion.11 = f32[8192]{0:T(1024)S(1)} fusion(f32[32768]{0:T(1024)S(1)} %bitcast.110, s32[8192]{0:T(1024)S(1)} %get-tuple-element.152), kind=kCustom, calls=%fused_computation.6.clone | custom fusion | bytes 98304 | tf_op jit(solution)/shard_map/jit(_take)/gather | solution.py:91
  742.1 45.5 %gather_fusion.8 = f32[8192]{0:T(1024)S(1)} fusion(f32[32768]{0:T(1024)S(1)} %bitcast.111, s32[8192]{0:T(1024)S(1)} %get-tuple-element.151), kind=kCustom, calls=%fused_computation.5.clone | custom fusion | bytes 98304 | tf_op jit(solution)/shard_map/jit(_take)/gather | solution.py:90
  788.3 9.4 psum.93
  797.7 32.9 %gather_fusion.13 = f32[8192]{0:T(1024)S(1)} fusion(f32[1024]{0:T(1024)S(1)} %fusion.55, s32[8192]{0:T(1024)S(1)} %get-tuple-element.157), kind=kCustom, calls=%fused_computation.14.clone | custom fusion | bytes 98304 | tf_op jit(solution)/shard_map/jit(_take)/gather | solution.py:92
  830.6 9.5 psum.94
  840.0 2.6 copy.38
  842.6 16.2 %psum.95 = f32[]{:T(128)} all-reduce(f32[]{:T(128)} %psum.94), channel_id=1, replica_groups=mesh['agent_0'=4,'agent_1'=4,'agent_2'=8,'grid'=2] {'agent_2'}, use_global_device_ids=true, to_apply=%region_24.27 | all-reduce | flops 1 | bytes 8 | tf_op jit(solution)/shard_map/psum | solution.py:38
  859.4 2.7 fusion.58
  862.1 45.5 %gather_fusion.15 = f32[8192]{0:T(1024)S(1)} fusion(f32[32768]{0:T(1024)S(1)} %bitcast.112, s32[8192]{0:T(1024)S(1)} %get-tuple-element.159), kind=kCustom, calls=%fused_computation.8.clone | custom fusion | bytes 98304 | tf_op jit(solution)/shard_map/jit(_take)/gather | solution.py:91
  907.7 45.5 %gather_fusion.12 = f32[8192]{0:T(1024)S(1)} fusion(f32[32768]{0:T(1024)S(1)} %bitcast.113, s32[8192]{0:T(1024)S(1)} %get-tuple-element.160), kind=kCustom, calls=%fused_computation.7.clone | custom fusion | bytes 98304 | tf_op jit(solution)/shard_map/jit(_take)/gather | solution.py:90
  (198 shorter events, 80.4 us)
Async XLA Ops:
  10.0 18.9 %copy-start.5 = (f32[4,16]{1,0:T(4,128)S(1)}, f32[4,16]{1,0:T(4,128)}, u32[]{:S(2)}) copy-start(f32[4,16]{1,0:T(4,128)} %param.22) | copy-start | bytes 772
  10.0 19.0 %copy-start.6 = (f32[4,16]{1,0:T(4,128)S(1)}, f32[4,16]{1,0:T(4,128)}, u32[]{:S(2)}) copy-start(f32[4,16]{1,0:T(4,128)} %param.21) | copy-start | bytes 772
  10.1 19.2 %copy-start.7 = (f32[32]{0:T(128)S(1)}, f32[32]{0:T(128)}, u32[]{:S(2)}) copy-start(f32[32]{0:T(128)} %param.23) | copy-start | bytes 388
  13.5 26.4 %all-to-all-start = ((f32[128,1,128]{2,1,0:T(1,128)}), f32[128,1,128]{2,1,0:T(1,128)S(1)}, u32[]{:S(2)}, u32[]{:S(2)}) async-start(f32[128,1,128]{2,1,0:T(1,128)} %reshape.401), calls=%async_computation | async-start | bytes 131072 | tf_op jit(solution)/shard_map/all_to_all | solution.py:127
  28.8 325.1 %all-gather.2.cloned.1.call-start = ((), (), s32[]{:S(2)}) async-start(), calls=%async_computation.2 | async-start | bytes 8454144 | tf_op jit(solution)/shard_map/all_gather | solution.py:145
  41.6 103.1 %copy-start.2 = (f32[8192]{0:T(1024)S(1)}, f32[8192]{0:T(1024)}, u32[]{:S(2)}) copy-start(f32[8192]{0:T(1024)} %param.24) | copy-start | bytes 98308
  41.6 138.5 %copy-start.4 = (s32[4]{0:T(128)S(1)}, s32[4]{0:T(128)}, u32[]{:S(2)}) copy-start(s32[4]{0:T(128)} %param.27) | copy-start | bytes 52
  41.7 144.3 %copy-start = (s32[4,8192]{1,0:T(4,128)S(1)}, s32[4,8192]{1,0:T(4,128)}, u32[]{:S(2)}) copy-start(s32[4,8192]{1,0:T(4,128)} %param.25) | copy-start | bytes 393220
  41.7 144.4 %copy-start.1 = (s32[4,8192]{1,0:T(4,128)S(1)}, s32[4,8192]{1,0:T(4,128)}, u32[]{:S(2)}) copy-start(s32[4,8192]{1,0:T(4,128)} %param.26) | copy-start | bytes 393220
  140.3 78.8 %copy-start.3 = (f32[16,512]{1,0:T(8,128)}, f32[16,512]{1,0:T(8,128)S(1)}, u32[]{:S(2)}) copy-start(f32[16,512]{1,0:T(8,128)S(1)} %get-tuple-element.49) | copy-start | bytes 98308
Sparse Core Ops, SparseCore 0:
  144.9 117.9 all-gather.1
where the time goes:
time: 964 us; the launch traced here: 961 us
  local copies, waits for them, and re-layouts  692 us (72%)
  blocking collectives  143 us (15%)
  other arithmetic  65.1 us (7%)
  between operations  24.8 us (3%)
  starting transfers between devices  15.4 us (2%)
  matrix products  10.4 us (1%)
  waiting for transfers between devices  10.4 us (1%)
    gather x4, local copies, waits for them, and re-layouts, advance(): value_high = jnp.take(flattened, flat_index + 1)  182 us
    gather x4, local copies, waits for them, and re-layouts, advance(): value_low = jnp.take(flattened, flat_index)  182 us
    psum x12, blocking collectives, over_axes(): x = lax.psum(x, axis)  139 us
    gather x4, local copies, waits for them, and re-layouts, advance(): edge_high = jnp.take(points, bracket_row + 1)  131 us
    gather x4, local copies, waits for them, and re-layouts, advance(): edge_low = jnp.take(points, bracket_row)  131 us
    dynamic_update_slice x32, local copies, waits for them, and re-layouts, on_device(): values_now, policy = lax.map(one_state, (expected, growth, income))  22 us
    reduce_sum x16, other arithmetic, bellman(): chosen = jnp.sum(weight * points[None, :], axis=1) / totals  21.9 us
    add x16, other arithmetic, one_state(): return bellman(points, own_points * factor + earned, column)  20.7 us
  transfers between devices with their start and end apart: 2, of which 1 were waited for; matrix products, arithmetic and copies ran while one was open for 17% of the time, Pallas kernels for 0%

commit v1 on v0

--- a/solution.py
+++ b/solution.py
@@ -35,7 +35,7 @@
 
 def over_axes(x, axes):
     for axis in axes:
-        x = lax.psum(x, axis)
+        x = jnp.sum(lax.all_gather(x, axis), axis=0)
     return x
 
 

time: 964 us -> 985 us (1.022)
  local copies, waits for them, and re-layouts: 692 us -> 711 us
    psum x12 -> x0, blocking collectives: 139 us -> none  [over_axes(): x = lax.psum(x, axis)]
    unnamed x0 -> x12, blocking collectives: none -> 133 us
    unnamed x23 -> x56, local copies, waits for them, and re-layouts: 13.3 us -> 32.1 us
  transfers between devices with their start and end apart: 2 -> 2, of which waited for: 1 -> 2; matrix products, arithmetic and copies ran while one was open for 17% -> 8% of each run, Pallas kernels for 0% -> 0%
where the time goes in v1:
time: 985 us; the launch traced here: 983 us
  local copies, waits for them, and re-layouts  711 us (72%)
  blocking collectives  137 us (14%)
  other arithmetic  72.3 us (7%)
  between operations  24.7 us (3%)
  starting transfers between devices  15.4 us (2%)
  waiting for transfers between devices  12.2 us (1%)
  matrix products  10.4 us (1%)
    gather x4, local copies, waits for them, and re-layouts, advance(): value_high = jnp.take(flattened, flat_index + 1)  182 us
    gather x4, local copies, waits for them, and re-layouts, advance(): value_low = jnp.take(flattened, flat_index)  182 us
    unnamed x12, blocking collectives  133 us
    gather x4, local copies, waits for them, and re-layouts, advance(): edge_high = jnp.take(points, bracket_row + 1)  131 us
    gather x4, local copies, waits for them, and re-layouts, advance(): edge_low = jnp.take(points, bracket_row)  131 us
    unnamed x56, local copies, waits for them, and re-layouts  32.1 us
    dynamic_update_slice x32, local copies, waits for them, and re-layouts, on_device(): values_now, policy = lax.map(one_state, (expected, growth, income))  22 us
    reduce_sum x16, other arithmetic, bellman(): chosen = jnp.sum(weight * points[None, :], axis=1) / totals  21.9 us
  transfers between devices with their start and end apart: 2, of which 2 were waited for; matrix products, arithmetic and copies ran while one was open for 8% of the time, Pallas kernels for 0%

profile of v1, /device:TPU:8, one launch (start us, length us, event | category | flops | bytes accessed | tf_op | source)
XLA Modules:
  0.0 982.7 jit_solution(15434179907295496186)
XLA Ops:
  13.5 15.3 %all-to-all-start = ((f32[128,1,128]{2,1,0:T(1,128)}), f32[128,1,128]{2,1,0:T(1,128)S(1)}, u32[]{:S(2)}, u32[]{:S(2)}) async-start(f32[128,1,128]{2,1,0:T(1,128)} %reshape.461), calls=%async_computation | async-start | bytes 131072 | tf_op jit(solution)/shard_map/all_to_all | solution.py:127
  29.6 10.3 %all-to-all-done = f32[128,1,128]{2,1,0:T(1,128)S(1)} async-done(((f32[128,1,128]{2,1,0:T(1,128)}), f32[128,1,128]{2,1,0:T(1,128)S(1)}, u32[]{:S(2)}, u32[]{:S(2)}) %all-to-all-start) | async-done | bytes 65568 | tf_op jit(solution)/shard_map/all_to_all | solution.py:127
  41.7 98.6 %while.14 = (s32[]{:T(128)}, f32[16,512]{1,0:T(8,128)}, f32[16,512]{1,0:T(8,128)S(1)}, f32[16]{0:T(128)S(1)}, f32[512]{0:T(512)S(1)}, /*index=5*/f32[16]{0:T(128)S(1)}, f32[16,1024]{1,0:T(8,128)S(1)}, s32[]{:T(128)}, s32[]{:T(128)}) while((s32[]{:T(128)}, f32[16,512]{1,0:T(8,128)}, f32[16,512]{1,0:T(8,128)S(1)}, ...), condition=%wide.region_8.9_spmd.clone.clone, body=%wide.region_4.8_spmd.clone.clone.sunk | while | flops 9966594 | bytes 63633 | solution.py:142
  45.1 1.4 multiply_reduce_fusion.2
  51.3 1.4 multiply_reduce_fusion.2
  57.4 1.4 multiply_reduce_fusion.2
  63.6 1.4 multiply_reduce_fusion.2
  69.8 1.4 multiply_reduce_fusion.2
  75.9 1.4 multiply_reduce_fusion.2
  82.1 1.4 multiply_reduce_fusion.2
  88.3 1.4 multiply_reduce_fusion.2
  94.4 1.4 multiply_reduce_fusion.2
  100.6 1.4 multiply_reduce_fusion.2
  106.7 1.4 multiply_reduce_fusion.2
  112.9 1.4 multiply_reduce_fusion.2
  119.1 1.4 multiply_reduce_fusion.2
  125.2 1.4 multiply_reduce_fusion.2
  131.4 1.4 multiply_reduce_fusion.2
  137.6 1.4 multiply_reduce_fusion.2
  140.4 3.8 all_to_all.24
  147.4 8.3 all-reduce
  157.0 1.4 dynamic-update-slice.1
  158.4 9.2 all-reduce.1
  168.9 1.4 dynamic-update-slice.2
  170.3 15.3 %all-reduce.2 = f32[8]{0:T(128)S(1)} all-reduce(f32[8]{0:T(128)S(1)} %dynamic-update-slice.2), channel_id=1, replica_groups=mesh['agent_0'=4,'agent_1'=4,'agent_2'=8,'grid'=2] {'agent_2'}, use_global_device_ids=true, to_apply=%add.2 | all-reduce | flops 8 | bytes 64
  191.5 32.9 %gather_fusion.2 = f32[8192]{0:T(1024)S(1)} fusion(f32[1024]{0:T(1024)S(1)} %fusion.55, s32[8192]{0:T(1024)S(1)} %get-tuple-element.165), kind=kCustom, calls=%fused_computation.9.clone | custom fusion | bytes 98304 | tf_op jit(solution)/shard_map/jit(_take)/gather | solution.py:93
  224.4 32.9 %gather_fusion.1 = f32[8192]{0:T(1024)S(1)} fusion(f32[1024]{0:T(1024)S(1)} %fusion.55, s32[8192]{0:T(1024)S(1)} %get-tuple-element.166), kind=kCustom, calls=%fused_computation.1.clone | custom fusion | bytes 98304 | tf_op jit(solution)/shard_map/jit(_take)/gather | solution.py:92
  261.2 1.8 all-gather.2.cloned.1.call-done
  263.0 6.7 constant_dynamic-slice_fusion.3
  272.1 45.5 %gather_fusion.3 = f32[8192]{0:T(1024)S(1)} fusion(f32[32768]{0:T(1024)S(1)} %bitcast.121, s32[8192]{0:T(1024)S(1)} %get-tuple-element.156), kind=kCustom, calls=%fused_computation.2.clone | custom fusion | bytes 98304 | tf_op jit(solution)/shard_map/jit(_take)/gather | solution.py:91
  317.6 45.5 %gather_fusion = f32[8192]{0:T(1024)S(1)} fusion(f32[32768]{0:T(1024)S(1)} %bitcast.122, s32[8192]{0:T(1024)S(1)} %get-tuple-element.155), kind=kCustom, calls=%fused_computation.clone | custom fusion | bytes 98304 | tf_op jit(solution)/shard_map/jit(_take)/gather | solution.py:90
  365.2 32.9 %gather_fusion.6 = f32[8192]{0:T(1024)S(1)} fusion(f32[1024]{0:T(1024)S(1)} %fusion.55, s32[8192]{0:T(1024)S(1)} %get-tuple-element.163), kind=kCustom, calls=%fused_computation.11.clone | custom fusion | bytes 98304 | tf_op jit(solution)/shard_map/jit(_take)/gather | solution.py:93
  398.1 9.2 all-reduce.3
  407.9 1.4 dynamic-update-slice.4
  409.3 32.9 %gather_fusion.5 = f32[8192]{0:T(1024)S(1)} fusion(f32[1024]{0:T(1024)S(1)} %fusion.55, s32[8192]{0:T(1024)S(1)} %get-tuple-element.164), kind=kCustom, calls=%fused_computation.10.clone | custom fusion | bytes 98304 | tf_op jit(solution)/shard_map/jit(_take)/gather | solution.py:92
  442.2 9.5 all-reduce.4
  452.3 1.4 dynamic-update-slice.5
  453.7 4.2 copy.36
  457.9 15.9 %all-reduce.5 = f32[8]{0:T(128)S(1)} all-reduce(f32[8]{0:T(128)S(1)} %dynamic-update-slice.5), channel_id=1, replica_groups=mesh['agent_0'=4,'agent_1'=4,'agent_2'=8,'grid'=2] {'agent_2'}, use_global_device_ids=true, to_apply=%add.5 | all-reduce | flops 8 | bytes 64
  475.0 2.7 fusion.62
  477.7 45.5 %gather_fusion.7 = f32[8192]{0:T(1024)S(1)} fusion(f32[32768]{0:T(1024)S(1)} %bitcast.123, s32[8192]{0:T(1024)S(1)} %get-tuple-element.154), kind=kCustom, calls=%fused_computation.4.clone | custom fusion | bytes 98304 | tf_op jit(solution)/shard_map/jit(_take)/gather | solution.py:91
  523.3 45.5 %gather_fusion.4 = f32[8192]{0:T(1024)S(1)} fusion(f32[32768]{0:T(1024)S(1)} %bitcast.124, s32[8192]{0:T(1024)S(1)} %get-tuple-element.153), kind=kCustom, calls=%fused_computation.3.clone | custom fusion | bytes 98304 | tf_op jit(solution)/shard_map/jit(_take)/gather | solution.py:90
  570.8 32.9 %gather_fusion.10 = f32[8192]{0:T(1024)S(1)} fusion(f32[1024]{0:T(1024)S(1)} %fusion.55, s32[8192]{0:T(1024)S(1)} %get-tuple-element.161), kind=kCustom, calls=%fused_computation.13.clone | custom fusion | bytes 98304 | tf_op jit(solution)/shard_map/jit(_take)/gather | solution.py:93
  603.7 7.7 all-reduce.6
  612.0 1.4 dynamic-update-slice.7
  613.5 32.9 %gather_fusion.9 = f32[8192]{0:T(1024)S(1)} fusion(f32[1024]{0:T(1024)S(1)} %fusion.55, s32[8192]{0:T(1024)S(1)} %get-tuple-element.162), kind=kCustom, calls=%fused_computation.12.clone | custom fusion | bytes 98304 | tf_op jit(solution)/shard_map/jit(_take)/gather | solution.py:92
  646.4 9.8 %all-reduce.7 = f32[4]{0:T(128)S(1)} all-reduce(f32[4]{0:T(128)S(1)} %dynamic-update-slice.7), channel_id=1, replica_groups=mesh['agent_0'=4,'agent_1'=4,'agent_2'=8,'grid'=2] {'agent_1'}, use_global_device_ids=true, to_apply=%add.7 | all-reduce | flops 4 | bytes 32
  656.8 1.5 dynamic-update-slice.8
  658.3 4.2 copy.37
  662.5 14.4 %all-reduce.8 = f32[8]{0:T(128)S(1)} all-reduce(f32[8]{0:T(128)S(1)} %dynamic-update-slice.8), channel_id=1, replica_groups=mesh['agent_0'=4,'agent_1'=4,'agent_2'=8,'grid'=2] {'agent_2'}, use_global_device_ids=true, to_apply=%add.8 | all-reduce | flops 8 | bytes 64
  678.1 2.7 fusion.60
  680.8 45.5 %gather_fusion.11 = f32[8192]{0:T(1024)S(1)} fusion(f32[32768]{0:T(1024)S(1)} %bitcast.125, s32[8192]{0:T(1024)S(1)} %get-tuple-element.152), kind=kCustom, calls=%fused_computation.6.clone | custom fusion | bytes 98304 | tf_op jit(solution)/shard_map/jit(_take)/gather | solution.py:91
  726.3 45.5 %gather_fusion.8 = f32[8192]{0:T(1024)S(1)} fusion(f32[32768]{0:T(1024)S(1)} %bitcast.126, s32[8192]{0:T(1024)S(1)} %get-tuple-element.151), kind=kCustom, calls=%fused_computation.5.clone | custom fusion | bytes 98304 | tf_op jit(solution)/shard_map/jit(_take)/gather | solution.py:90
  773.9 32.9 %gather_fusion.14 = f32[8192]{0:T(1024)S(1)} fusion(f32[1024]{0:T(1024)S(1)} %fusion.55, s32[8192]{0:T(1024)S(1)} %get-tuple-element.158), kind=kCustom, calls=%fused_computation.15.clone | custom fusion | bytes 98304 | tf_op jit(solution)/shard_map/jit(_take)/gather | solution.py:93
  806.8 8.5 all-reduce.9
  815.9 1.4 dynamic-update-slice.10
  817.4 32.9 %gather_fusion.13 = f32[8192]{0:T(1024)S(1)} fusion(f32[1024]{0:T(1024)S(1)} %fusion.55, s32[8192]{0:T(1024)S(1)} %get-tuple-element.157), kind=kCustom, calls=%fused_computation.14.clone | custom fusion | bytes 98304 | tf_op jit(solution)/shard_map/jit(_take)/gather | solution.py:92
  850.2 8.9 all-reduce.10
  859.7 1.4 dynamic-update-slice.11
  861.1 2.6 copy.38
  863.7 15.9 %all-reduce.11 = f32[8]{0:T(128)S(1)} all-reduce(f32[8]{0:T(128)S(1)} %dynamic-update-slice.11), channel_id=1, replica_groups=mesh['agent_0'=4,'agent_1'=4,'agent_2'=8,'grid'=2] {'agent_2'}, use_global_device_ids=true, to_apply=%add.11 | all-reduce | flops 8 | bytes 64
  880.8 2.7 fusion.58
  883.5 45.5 %gather_fusion.15 = f32[8192]{0:T(1024)S(1)} fusion(f32[32768]{0:T(1024)S(1)} %bitcast.127, s32[8192]{0:T(1024)S(1)} %get-tuple-element.159), kind=kCustom, calls=%fused_computation.8.clone | custom fusion | bytes 98304 | tf_op jit(solution)/shard_map/jit(_take)/gather | solution.py:91
  929.1 45.5 %gather_fusion.12 = f32[8192]{0:T(1024)S(1)} fusion(f32[32768]{0:T(1024)S(1)} %bitcast.128, s32[8192]{0:T(1024)S(1)} %get-tuple-element.160), kind=kCustom, calls=%fused_computation.7.clone | custom fusion | bytes 98304 | tf_op jit(solution)/shard_map/jit(_take)/gather | solution.py:90
  (243 shorter events, 107.1 us)
Async XLA Ops:
  10.0 18.9 %copy-start.5 = (f32[4,16]{1,0:T(4,128)S(1)}, f32[4,16]{1,0:T(4,128)}, u32[]{:S(2)}) copy-start(f32[4,16]{1,0:T(4,128)} %param.22) | copy-start | bytes 772
  10.0 19.0 %copy-start.6 = (f32[4,16]{1,0:T(4,128)S(1)}, f32[4,16]{1,0:T(4,128)}, u32[]{:S(2)}) copy-start(f32[4,16]{1,0:T(4,128)} %param.21) | copy-start | bytes 772
  10.1 19.2 %copy-start.7 = (f32[32]{0:T(128)S(1)}, f32[32]{0:T(128)}, u32[]{:S(2)}) copy-start(f32[32]{0:T(128)} %param.23) | copy-start | bytes 388
  13.5 26.4 %all-to-all-start = ((f32[128,1,128]{2,1,0:T(1,128)}), f32[128,1,128]{2,1,0:T(1,128)S(1)}, u32[]{:S(2)}, u32[]{:S(2)}) async-start(f32[128,1,128]{2,1,0:T(1,128)} %reshape.461), calls=%async_computation | async-start | bytes 131072 | tf_op jit(solution)/shard_map/all_to_all | solution.py:127
  28.8 234.2 %all-gather.2.cloned.1.call-start = ((), (), s32[]{:S(2)}) async-start(), calls=%async_computation.2 | async-start | bytes 8454144 | tf_op jit(solution)/shard_map/all_gather | solution.py:145
  41.6 103.2 %copy-start.2 = (f32[8192]{0:T(1024)S(1)}, f32[8192]{0:T(1024)}, u32[]{:S(2)}) copy-start(f32[8192]{0:T(1024)} %param.24) | copy-start | bytes 98308
  41.6 103.8 %copy-start.10 = (u32[256]{0:T(256)S(1)}, u32[256]{0:T(256)}, u32[]{:S(2)}) copy-start(u32[256]{0:T(256)} %constant.175) | copy-start | bytes 3076
  41.7 114.1 %copy-start.9 = (u32[256]{0:T(256)S(1)}, u32[256]{0:T(256)}, u32[]{:S(2)}) copy-start(u32[256]{0:T(256)} %constant.180) | copy-start | bytes 3076
  41.7 126.0 %copy-start.8 = (u32[256]{0:T(256)S(1)}, u32[256]{0:T(256)}, u32[]{:S(2)}) copy-start(u32[256]{0:T(256)} %constant.185) | copy-start | bytes 3076
  41.7 143.9 %copy-start.4 = (s32[4]{0:T(128)S(1)}, s32[4]{0:T(128)}, u32[]{:S(2)}) copy-start(s32[4]{0:T(128)} %param.27) | copy-start | bytes 52
  41.7 149.6 %copy-start = (s32[4,8192]{1,0:T(4,128)S(1)}, s32[4,8192]{1,0:T(4,128)}, u32[]{:S(2)}) copy-start(s32[4,8192]{1,0:T(4,128)} %param.25) | copy-start | bytes 393220
  41.7 149.7 %copy-start.1 = (s32[4,8192]{1,0:T(4,128)S(1)}, s32[4,8192]{1,0:T(4,128)}, u32[]{:S(2)}) copy-start(s32[4,8192]{1,0:T(4,128)} %param.26) | copy-start | bytes 393220
  140.3 84.1 %copy-start.3 = (f32[16,512]{1,0:T(8,128)}, f32[16,512]{1,0:T(8,128)S(1)}, u32[]{:S(2)}) copy-start(f32[16,512]{1,0:T(8,128)S(1)} %get-tuple-element.49) | copy-start | bytes 98308
Sparse Core Ops, SparseCore 0:
  144.9 118.0 all-gather.1
